TPU v7x, 32 devices: a whole 2x2x4 slice. The times are simulated.
32 devices in a mesh: cat: 2 (over x), lat: 4 (over y, core), lon: 4 (over z).
Axes of the slice: x: 2, y: 2, z: 4, core: 2. Of those that a mesh axis runs over, the one named last changes fastest.
Arguments:
- thickness: bfloat16 [40, 1024, 2560], P('cat', 'lat', 'lon'), may hold values from 0.099609375 to 4
- area: bfloat16 [40, 1024, 2560], P('cat', 'lat', 'lon'), may hold values from 0.0049743652 to 0.049804688
- ridge_weight: float32 [40], P('cat'), may hold values from 0.2 to 2
- cat_top: int32 [1024, 2560], P('lat', 'lon'), may hold values from 1 to 40
- land_mask: int32 [1024, 2560], P('lat', 'lon'), may hold values 0 or 1
- velocity_u: float32 [1024, 2560], P('lat', 'lon'), may hold values from -1.8 to 1.8
- velocity_v: float32 [1024, 2560], P('lat', 'lon'), may hold values from -1.8 to 1.8
- stress_div: float32 [1024, 2560], P('lat', 'lon'), may hold values from -3 to 3
- stress_ten: float32 [1024, 2560], P('lat', 'lon'), may hold values from -3 to 3
- stress_shear: float32 [1024, 2560], P('lat', 'lon'), may hold values from -3 to 3
- wind_x: float32 [1024, 2560], P('lat', 'lon'), may hold values from -6 to 6
- wind_y: float32 [1024, 2560], P('lat', 'lon'), may hold values from -6 to 6
- water_drag: float32 [1024, 2560], P('lat', 'lon'), may hold values from 0.2 to 2
Outputs:
- new_u: float32 [1024, 2560], P('lat', 'lon')
- new_v: float32 [1024, 2560], P('lat', 'lon')
- new_div: float32 [1024, 2560], P('lat', 'lon')
- new_ten: float32 [1024, 2560], P('lat', 'lon')
- new_shear: float32 [1024, 2560], P('lat', 'lon')
Inputs may be any that keep to these rules, and one draw needn't show every extreme that they name: Categories with index cat_top or above are absent from a cell.
All inputs are finite; a program needn't handle non-finite values. No bound on the sum of `land_mask` on one device may be relied on, other than what follows from the above.
Results may differ from a plain program's by a relative error of at most 0.0003.
Values sent between devices are 32-bit elements; how exact they have to be, the bound alone decides.
A program may use at most 128 MiB of HBM per device.

v0:
```python
import jax
import jax.numpy as jnp
from jax import lax
from jax.sharding import PartitionSpec as P

SUB = 4


ELASTIC = 2.0
ECC_SQUARED = 4.0
DELTA_FLOOR = 0.05
CORIOLIS = 0.5


def extended(cells, sides, width, closed):
    for axis, dim in sides:
        count = lax.axis_size(axis)
        ends = count if closed else count - 1
        head = lax.slice_in_dim(cells, 0, width, axis=dim)
        tail = lax.slice_in_dim(cells, cells.shape[dim] - width, cells.shape[dim], axis=dim)
        cells = jnp.concatenate(
            [
                lax.ppermute(tail, axis, [(i, (i + 1) % count) for i in range(ends)]),
                cells,
                lax.ppermute(head, axis, [((i + 1) % count, i) for i in range(ends)]),
            ],
            axis=dim,
        )
    return cells


def slopes(along, across):
    return (
        0.5 * (along[:, :, 2:] - along[:, :, :-2]),
        0.5 * (across[:, 2:, :] - across[:, :-2, :]),
    )


def local_pad(along_stack, across_stack):
    along = jnp.pad(along_stack, ((0, 0), (0, 0), (1, 1)))
    across = jnp.pad(across_stack, ((0, 0), (1, 1), (0, 0)))
    return (along, across)


def subcycle(velocity, stresses, statics, velocity_pad, stress_pad):
    strength, mass, concentration, drag, push_x, push_y, wet = statics
    along, across = velocity_pad(velocity, velocity)
    ddx, ddy = slopes(along, across)
    divergence = ddx[0] + ddy[1]
    tension = ddx[0] - ddy[1]
    shearing = ddy[0] + ddx[1]
    delta = jnp.sqrt(
        divergence * divergence
        + (tension * tension + shearing * shearing) / ECC_SQUARED
        + DELTA_FLOOR * DELTA_FLOOR
    )
    relax = 1.0 / (1.0 + ELASTIC)
    viscous = ELASTIC * strength / delta
    first = wet * (stresses[0] + viscous * (divergence - delta)) * relax
    second = wet * (stresses[1] + viscous * tension / ECC_SQUARED) * relax
    cross = wet * (stresses[2] + viscous * shearing / ECC_SQUARED) * relax
    normal_x = 0.5 * (first + second)
    normal_y = 0.5 * (first - second)
    along_s, across_s = stress_pad(jnp.stack([normal_x, cross]), jnp.stack([cross, normal_y]))
    sdx, sdy = slopes(along_s, across_s)
    force_x = sdx[0] + sdy[0]
    force_y = sdx[1] + sdy[1]
    denom = mass + drag + 1.0 - wet
    speed_u = (
        wet
        * (mass * velocity[0] + force_x + concentration * push_x + CORIOLIS * mass * velocity[1])
        / denom
    )
    speed_v = (
        wet
        * (mass * velocity[1] + force_y + concentration * push_y - CORIOLIS * mass * velocity[0])
        / denom
    )
    return (jnp.stack([speed_u, speed_v]), jnp.stack([first, second, cross]))


def shards(
    thickness,
    area,
    ridge_weight,
    cat_top,
    land_mask,
    velocity_u,
    velocity_v,
    stress_div,
    stress_ten,
    stress_shear,
    wind_x,
    wind_y,
    water_drag,
):
    local_cats = thickness.shape[0]
    level = lax.axis_index("cat") * local_cats + lax.broadcasted_iota(jnp.int32, thickness.shape, 0)
    present = (level < cat_top[None]).astype(jnp.float32)
    height = thickness.astype(jnp.float32)
    cover = area.astype(jnp.float32) * present
    weighted = ridge_weight[:, None, None] * cover * height * height
    strength, mass, concentration = lax.psum(
        (jnp.sum(weighted, axis=0), jnp.sum(cover * height, axis=0), jnp.sum(cover, axis=0)), "cat"
    )
    wet = land_mask.astype(jnp.float32)
    margin = 2 * SUB
    bundle = jnp.stack(
        [
            strength,
            mass,
            concentration,
            water_drag,
            wind_x,
            wind_y,
            wet,
            velocity_u,
            velocity_v,
            stress_div,
            stress_ten,
            stress_shear,
        ]
    )
    widened = extended(bundle, (("lon", 2),), margin, True)
    padded = extended(widened, (("lat", 1),), margin, False)
    statics = tuple((padded[index] for index in range(7)))
    velocity = padded[7:9]
    stresses = padded[9:12]
    for step in range(SUB):
        velocity, stresses = subcycle(velocity, stresses, statics, local_pad, local_pad)
    rows = velocity.shape[1] - margin
    cols = velocity.shape[2] - margin
    velocity = velocity[:, margin:rows, margin:cols]
    stresses = stresses[:, margin:rows, margin:cols]
    return (velocity[0], velocity[1], stresses[0], stresses[1], stresses[2])


def solution(mesh):
    return jax.shard_map(
        shards,
        mesh=mesh,
        in_specs=(
            P("cat", "lat", "lon"),
            P("cat", "lat", "lon"),
            P("cat"),
            P("lat", "lon"),
            P("lat", "lon"),
            P("lat", "lon"),
            P("lat", "lon"),
            P("lat", "lon"),
            P("lat", "lon"),
            P("lat", "lon"),
            P("lat", "lon"),
            P("lat", "lon"),
            P("lat", "lon"),
        ),
        out_specs=(
            P("lat", "lon"),
            P("lat", "lon"),
            P("lat", "lon"),
            P("lat", "lon"),
            P("lat", "lon"),
        ),
        check_vma=False,
    )
```

profile of v0, /device:TPU:1, one launch (start us, length us, event | category | flops | bytes accessed | tf_op | source)
XLA Modules:
  0.0 152.7 jit_solution(10961664660529904791)
XLA Ops:
  7.2 9.6 %fusion = (f32[256,640]{1,0:T(8,128)}, f32[256,640]{1,0:T(8,128)}, f32[256,640]{1,0:T(8,128)}) fusion(bf16[20,256,640]{2,1,0:T(8,128)(2,1)} %param.13, bf16[20,256,640]{2,1,0:T(8,128)(2,1)} %param.14, s32[256,640]{1,0:T(8,128)} %param.16, s32[20]{0:T(128)S(1)} %iota_add_fusion, f32[20]{0:T(128)} %param.15), kind=kLoop, calls=%fused_computation.2 | loop fusion | flops 35553280 | bytes 15728800 | tf_op jit(solution)/shard_map/reduce_sum | solution.py:104
  16.9 62.2 %all-reduce.19.cloned.1.call-done = (f32[1,256,640]{2,1,0:T(8,128)}, f32[1,256,640]{2,1,0:T(8,128)}, f32[1,256,640]{2,1,0:T(8,128)}) async-done(((f32[1,256,640]{2,1,0:T(8,128)}, f32[1,256,640]{2,1,0:T(8,128)}, f32[1,256,640]{2,1,0:T(8,128)}), (f32[1,256,640]{2,1,0:T(8,128)}, f32[1,256,640]{2,1,0:T(8,128)}, f32[1,256,640]{2,1,0:T(8,128)})) %all-reduce.19.cloned.1.call-update) | async-done | bytes 1966096 | tf_op jit(solution)/shard_map/psum | solution.py:103
  79.1 1.3 constant_dynamic-update-slice_fusion.2
  80.6 0.1 copy-done.3
  80.8 0.7 copy-done.4
  81.8 0.2 copy-done.6
  82.0 0.8 copy-done.7
  83.0 0.2 copy-done.9
  83.2 0.8 copy-done.10
  84.0 0.1 copy-done.11
  84.2 3.0 %copy-done = f32[12,256,640]{2,1,0:T(8,128)} copy-done((f32[12,256,640]{2,1,0:T(8,128)}, f32[12,256,640]{2,1,0:T(8,128)S(1)}, u32[]{:S(2)}) %copy-start) | copy-done | bytes 7864344
  87.2 0.5 fusion.68
  87.7 0.4 copy.32
  88.2 1.2 collective-permute-start
  89.4 0.4 copy.33
  89.8 2.1 %collective-permute-start.1 = (f32[12,256,8]{1,2,0:T(8,128)S(1)}, f32[12,256,8]{1,2,0:T(8,128)S(1)}, u32[]{:S(2)}, u32[]{:S(2)}) collective-permute-start(f32[12,256,8]{1,2,0:T(8,128)S(1)} %copy.33), channel_id=1, source_target_pairs={{1,0},{2,1},{3,2},{0,3},{5,4},{6,5},{7,6},{4,7},{9,8},{10,9},{11,1... | collective-permute-start | bytes 294920 | tf_op jit(solution)/shard_map/ppermute | solution.py:25
  91.9 1.6 %collective-permute-done = f32[12,256,8]{1,2,0:T(8,128)S(1)} collective-permute-done((f32[12,256,8]{1,2,0:T(8,128)S(1)}, f32[12,256,8]{1,2,0:T(8,128)S(1)}, u32[]{:S(2)}, u32[]{:S(2)}) %collective-permute-start) | collective-permute-done | bytes 98336 | tf_op jit(solution)/shard_map/ppermute | solution.py:23
  93.6 0.5 copy.34
  94.0 2.4 %collective-permute-done.1 = f32[12,256,8]{1,2,0:T(8,128)S(1)} collective-permute-done((f32[12,256,8]{1,2,0:T(8,128)S(1)}, f32[12,256,8]{1,2,0:T(8,128)S(1)}, u32[]{:S(2)}, u32[]{:S(2)}) %collective-permute-start.1) | collective-permute-done | bytes 98336 | tf_op jit(solution)/shard_map/ppermute | solution.py:25
  96.4 0.5 copy.35
  96.9 1.3 pad_maximum_fusion.6
  98.2 3.8 %collective-permute-start.2 = (f32[12,8,656]{2,1,0:T(8,128)S(1)}, f32[12,8,656]{2,1,0:T(8,128)S(1)}, u32[]{:S(2)}, u32[]{:S(2)}) collective-permute-start(f32[12,8,656]{2,1,0:T(8,128)S(1)} %get-tuple-element.48), channel_id=1, source_target_pairs={{0,4},{4,8},{8,12},{1,5},{5,9},{9,13},{2,6},{6,10},{10,14},{3,7},{... | collective-permute-start | bytes 755720 | tf_op jit(solution)/shard_map/ppermute | solution.py:23
  102.0 1.9 %collective-permute-start.3 = (f32[12,8,656]{2,1,0:T(8,128)S(1)}, f32[12,8,656]{2,1,0:T(8,128)S(1)}, u32[]{:S(2)}, u32[]{:S(2)}) collective-permute-start(f32[12,8,656]{2,1,0:T(8,128)S(1)} %get-tuple-element.49), channel_id=1, source_target_pairs={{4,0},{8,4},{12,8},{5,1},{9,5},{13,9},{6,2},{10,6},{14,10},{7,3},{... | collective-permute-start | bytes 755720 | tf_op jit(solution)/shard_map/ppermute | solution.py:25
  103.9 1.7 %collective-permute-done.2 = f32[12,8,656]{2,1,0:T(8,128)S(1)} collective-permute-done((f32[12,8,656]{2,1,0:T(8,128)S(1)}, f32[12,8,656]{2,1,0:T(8,128)S(1)}, u32[]{:S(2)}, u32[]{:S(2)}) %collective-permute-start.2) | collective-permute-done | bytes 251936 | tf_op jit(solution)/shard_map/ppermute | solution.py:23
  105.6 4.4 %collective-permute-done.3 = f32[12,8,656]{2,1,0:T(8,128)S(1)} collective-permute-done((f32[12,8,656]{2,1,0:T(8,128)S(1)}, f32[12,8,656]{2,1,0:T(8,128)S(1)}, u32[]{:S(2)}, u32[]{:S(2)}) %collective-permute-start.3) | collective-permute-done | bytes 251936 | tf_op jit(solution)/shard_map/ppermute | solution.py:25
  110.0 6.5 %pad_maximum_fusion = f32[12,272,656]{2,1,0:T(8,128)S(1)} fusion(f32[12,8,656]{2,1,0:T(8,128)S(1)} %collective-permute-done.3, f32[12,256,8]{2,1,0:T(8,128)S(1)} %copy.35, f32[12,256,640]{2,1,0:T(8,128)} %copy-done, f32[12,256,8]{2,1,0:T(8,128)S(1)} %copy.34, f32[12,8,656]{2,1,0:T(8,128)S(1)} %collective-permute-done.2), kind=kLoop, calls=%fused_computation.6 | loop fusion | flops 8564736 | bytes 17129472 | tf_op jit(solution)/shard_map/concatenate | solution.py:21
  116.6 1.2 subtract_multiply_fusion.7
  117.8 0.9 add_multiply_fusion.3
  118.7 0.4 fusion.46
  119.1 0.5 select_maximum_fusion.7
  119.6 0.5 fusion.11
  120.1 0.1 select_maximum_fusion.3
  120.3 0.2 fusion.10
  120.5 0.5 fusion.44
  121.0 0.5 fusion.37
  121.6 1.2 subtract_multiply_fusion.5
  122.8 1.6 %multiply_multiply_fusion.2 = (f32[1,272,656]{2,1,0:T(8,128)}, f32[1,272,656]{2,1,0:T(8,128)S(1)}) fusion(f32[12,272,656]{2,1,0:T(8,128)S(1)} %pad_maximum_fusion, f32[1,272,656]{2,1,0:T(8,128)S(1)} %get-tuple-element.41, f32[2,272,656]{2,1,0:T(8,128)S(1)} %get-tuple-element.68, f32[2,272,656]{2,1,0:T(8,128)S(1)} %get-tuple-element.67, ...), kind=kLoop, calls=%fused_computation.101 | loop fusion | flops 4282368 | bytes 8564736 | tf_op jit(solution)/shard_map/mul | solution.py:60
  124.4 0.9 add_multiply_fusion.2
  125.3 0.5 select_maximum_fusion.6
  125.8 0.5 fusion.9
  126.4 0.1 select_maximum_fusion.2
  126.5 0.2 fusion.8
  126.8 0.6 fusion.32
  127.5 1.2 subtract_multiply_fusion.3
  128.7 1.3 multiply_multiply_fusion.1
  130.0 1.1 add_multiply_fusion.1
  131.1 0.5 select_maximum_fusion.5
  131.6 0.5 fusion.7
  132.2 0.1 select_maximum_fusion.1
  132.4 0.2 fusion.6
  132.6 0.6 fusion.22
  133.3 1.2 subtract_multiply_fusion.1
  134.5 0.9 add_multiply_fusion
  135.4 0.3 multiply_multiply_fusion.3
  135.7 1.1 slice_bitcast_fusion
  136.8 1.1 slice_bitcast_fusion.1
  138.0 0.5 select_maximum_fusion.4
  138.5 0.5 fusion.5
  139.1 0.1 select_maximum_fusion
  139.2 0.2 fusion.4
  139.6 1.0 copy-done.1
  140.6 0.3 copy-done.2
  140.9 1.8 %fusion.53 = f32[256,640]{1,0:T(8,128)} fusion(f32[1,272,656]{2,1,0:T(8,128)S(1)} %get-tuple-element.24, f32[1,272,656]{2,1,0:T(8,128)S(1)} %get-tuple-element.26, f32[1,272,656]{2,1,0:T(8,128)S(1)} %copy-done.2, f32[1,272,656]{2,1,0:T(8,128)S(1)} %copy-done.1, f32[1,272,656]{2,1,0:T(8,128)S(1)} %get-tuple-element.50), kind=kLoop, calls=%fused_computation.146 | loop fusion | flops 1310720 | bytes 3932160 | tf_op jit(solution)/shard_map/squeeze | solution.py:135
  142.6 3.2 %fusion.59 = (f32[256,640]{1,0:T(8,128)}, f32[256,640]{1,0:T(8,128)}) fusion(f32[1,272,656]{2,1,0:T(8,128)S(1)} %get-tuple-element.37, f32[1,272,656]{2,1,0:T(8,128)S(1)} %get-tuple-element.59, f32[1,272,656]{2,1,0:T(8,128)S(1)} %get-tuple-element.57, f32[1,272,656]{2,1,0:T(8,128)S(1)} %get-tuple-element.34, f32[1,272,656]{2,1,0:T(8,128)S(1)} %get-tuple-element.43, ...), kind=kLoop, calls=%fused_computation.155 | loop fusion | flops 2621440 | bytes 9175040 | tf_op jit(solution)/shard_map/squeeze | solution.py:135
  (41 shorter events, 1.9 us)
Async XLA Ops:
  7.2 71.9 %all-reduce.19.cloned.1.call-start = ((), (), s32[]{:S(2)}) async-start(), calls=%async_computation | async-start | bytes 3932160 | tf_op jit(solution)/shard_map/psum | solution.py:103
  79.1 1.3 copy-start.13
  79.1 1.5 copy-start.12
  79.1 1.7 %copy-start.3 = (f32[256,640]{1,0:T(8,128)S(1)}, f32[256,640]{1,0:T(8,128)}, u32[]{:S(2)}) copy-start(f32[256,640]{1,0:T(8,128)} %param.25) | copy-start | bytes 1966084
  80.4 1.2 copy-start.4
  80.6 1.2 copy-start.5
  80.8 1.2 copy-start.6
  81.6 1.2 copy-start.7
  81.7 1.2 copy-start.8
  81.9 1.2 copy-start.9
  82.7 1.2 copy-start.10
  82.9 1.2 copy-start.11
  84.1 3.1 %copy-start = (f32[12,256,640]{2,1,0:T(8,128)}, f32[12,256,640]{2,1,0:T(8,128)S(1)}, u32[]{:S(2)}) copy-start(f32[12,256,640]{2,1,0:T(8,128)S(1)} %bitcast_dynamic-update-slice_fusion) | copy-start | bytes 23592964
  88.2 5.4 %collective-permute-start = (f32[12,256,8]{1,2,0:T(8,128)S(1)}, f32[12,256,8]{1,2,0:T(8,128)S(1)}, u32[]{:S(2)}, u32[]{:S(2)}) collective-permute-start(f32[12,256,8]{1,2,0:T(8,128)S(1)} %copy.32), channel_id=1, source_target_pairs={{0,1},{1,2},{2,3},{3,0},{4,5},{5,6},{6,7},{7,4},{8,9},{9,10},{10,1... | collective-permute-start | bytes 294920 | tf_op jit(solution)/shard_map/ppermute | solution.py:23
  89.8 6.6 %collective-permute-start.1 = (f32[12,256,8]{1,2,0:T(8,128)S(1)}, f32[12,256,8]{1,2,0:T(8,128)S(1)}, u32[]{:S(2)}, u32[]{:S(2)}) collective-permute-start(f32[12,256,8]{1,2,0:T(8,128)S(1)} %copy.33), channel_id=1, source_target_pairs={{1,0},{2,1},{3,2},{0,3},{5,4},{6,5},{7,6},{4,7},{9,8},{10,9},{11,1... | collective-permute-start | bytes 294920 | tf_op jit(solution)/shard_map/ppermute | solution.py:25
  98.2 7.4 %collective-permute-start.2 = (f32[12,8,656]{2,1,0:T(8,128)S(1)}, f32[12,8,656]{2,1,0:T(8,128)S(1)}, u32[]{:S(2)}, u32[]{:S(2)}) collective-permute-start(f32[12,8,656]{2,1,0:T(8,128)S(1)} %get-tuple-element.48), channel_id=1, source_target_pairs={{0,4},{4,8},{8,12},{1,5},{5,9},{9,13},{2,6},{6,10},{10,14},{3,7},{... | collective-permute-start | bytes 755720 | tf_op jit(solution)/shard_map/ppermute | solution.py:23
  102.0 8.0 %collective-permute-start.3 = (f32[12,8,656]{2,1,0:T(8,128)S(1)}, f32[12,8,656]{2,1,0:T(8,128)S(1)}, u32[]{:S(2)}, u32[]{:S(2)}) collective-permute-start(f32[12,8,656]{2,1,0:T(8,128)S(1)} %get-tuple-element.49), channel_id=1, source_target_pairs={{4,0},{8,4},{12,8},{5,1},{9,5},{13,9},{6,2},{10,6},{14,10},{7,3},{... | collective-permute-start | bytes 755720 | tf_op jit(solution)/shard_map/ppermute | solution.py:25
  139.4 1.2 copy-start.1
  139.5 1.4 copy-start.2
Sparse Core Ops, SparseCore 0:
  17.0 62.0 all-reduce.18
where the time goes:
time: 153 us
  waiting for transfers between devices  72.3 us (47%)
  other arithmetic  42.8 us (28%)
  between operations  14.4 us (9%)
  local copies, waits for them, and re-layouts  14.1 us (9%)
  starting transfers between devices  9.05 us (6%)
    psum x1, waiting for transfers between devices, shards(): lax.psum((jnp.sum(weighted, axis=0), jnp.sum(cover * height, axis=0), jnp...  62.2 us
    reduce_sum x1, other arithmetic, shards(): jnp.sum(cover * height, axis=0)  9.63 us
    unnamed x38, local copies, waits for them, and re-layouts  9.22 us
    mul x8, other arithmetic, slopes(): 0.5 * (along[:, :, 2:] - along[:, :, :-2])  6.78 us
    ppermute x2, waiting for transfers between devices, extended(): lax.ppermute(head, axis, [((i + 1) % count, i) for i in range(ends)])  6.75 us
    concatenate x1, other arithmetic, extended(): jnp.concatenate([lax.ppermute(tail, axis, [(i, (i + 1) % count) for i in...  6.47 us
    ppermute x2, starting transfers between devices, extended(): lax.ppermute(tail, axis, [(i, (i + 1) % count) for i in range(ends)])  5.01 us
    squeeze x2, other arithmetic, shards(): return (velocity[0], velocity[1], stresses[0], stresses[1], stresses[2])  4.95 us
  transfers between devices with their start and end apart: 5, of which 5 were waited for; matrix products, arithmetic and copies ran while one was open for 1% of the time, Pallas kernels for 0%

commit v1 on v0

v1 whole, which is shorter than its diff:
```python
import functools

import jax
import jax.numpy as jnp
from jax import lax
from jax.experimental import pallas as pl
from jax.experimental.pallas import tpu as pltpu
from jax.sharding import PartitionSpec as P

SUB = 4
LANES = 128
EDGE = 8
CHUNK = 32
BLOCK = 16
TOP = 24
MESH = pl.DeviceIdType.MESH

FS, FM, FC, FD, FX, FY, FW, FU, FV, F1, F2, F3 = range(12)
FIELDS = 12


def kernel(
    lat_count,
    lon_count,
    weight,
    thick_hbm,
    area_hbm,
    top_hbm,
    land_hbm,
    u_hbm,
    v_hbm,
    s1_hbm,
    s2_hbm,
    s3_hbm,
    wx_hbm,
    wy_hbm,
    drag_hbm,
    out_u,
    out_v,
    out_1,
    out_2,
    out_3,
    field,
    own,
    other,
    thick,
    area,
    top,
    land,
    pack_left,
    pack_right,
    from_left,
    from_right,
    load_sem,
    x_send,
    x_recv,
    halo_send,
    halo_recv,
    out_sem,
):
    cats, rows, cols = thick.shape
    wide = cols + LANES
    last = cols - LANES
    middle = cols - 2 * LANES
    events = (rows - 2 * BLOCK) // CHUNK
    my_cat = lax.axis_index("cat")
    my_lat = lax.axis_index("lat")
    my_lon = lax.axis_index("lon")
    partner = {"cat": 1 - my_cat}
    west = {"lon": lax.rem(my_lon + lon_count - 1, lon_count)}
    east = {"lon": lax.rem(my_lon + 1, lon_count)}
    north = {"lat": my_lat - 1}
    south = {"lat": my_lat + 1}
    has_north = my_lat > 0
    has_south = my_lat < lat_count - 1

    top_load = pltpu.make_async_copy(top_hbm, top, load_sem.at[0])
    top_load.start()
    strips = ((0, LANES), (last, LANES), (LANES, middle))
    cat_loads = []
    for k, (c0, w) in enumerate(strips):
        pair = (
            pltpu.make_async_copy(
                thick_hbm.at[:, :, pl.ds(c0, w)], thick.at[:, :, pl.ds(c0, w)], load_sem.at[1 + 2 * k]
            ),
            pltpu.make_async_copy(
                area_hbm.at[:, :, pl.ds(c0, w)], area.at[:, :, pl.ds(c0, w)], load_sem.at[2 + 2 * k]
            ),
        )
        for copy in pair:
            copy.start()
        cat_loads.append(pair)
    land_load = pltpu.make_async_copy(land_hbm, land, load_sem.at[7])
    land_load.start()
    field_loads = []
    for k, (f, ref) in enumerate(
        (
            (FU, u_hbm),
            (FV, v_hbm),
            (F1, s1_hbm),
            (F2, s2_hbm),
            (F3, s3_hbm),
            (FX, wx_hbm),
            (FY, wy_hbm),
            (FD, drag_hbm),
        )
    ):
        copy = pltpu.make_async_copy(
            ref, field.at[f, pl.ds(TOP, rows), pl.ds(0, cols)], load_sem.at[8 + k]
        )
        copy.start()
        field_loads.append(copy)

    barrier = pltpu.get_barrier_semaphore()
    for device in (partner, west, east):
        pl.semaphore_signal(barrier, inc=1, device_id=device, device_id_type=MESH)

    @pl.when(has_north)
    def _():
        pl.semaphore_signal(barrier, inc=1, device_id=north, device_id_type=MESH)

    @pl.when(has_south)
    def _():
        pl.semaphore_signal(barrier, inc=1, device_id=south, device_id_type=MESH)

    @pl.when(jnp.logical_not(has_north))
    def _():
        field[:, pl.ds(TOP - EDGE, EDGE), :] = jnp.zeros((FIELDS, EDGE, wide), jnp.float32)

    @pl.when(jnp.logical_not(has_south))
    def _():
        field[:, pl.ds(TOP + rows, EDGE), :] = jnp.zeros((FIELDS, EDGE, wide), jnp.float32)

    base = my_cat * cats

    def partial(r0, count, c0, w):
        def body(i, carry):
            r = pl.multiple_of(r0 + i * BLOCK, BLOCK)
            for c in range(c0, c0 + w, LANES):
                lanes = pl.ds(c, LANES)
                limit = top[pl.ds(r, BLOCK), lanes] - base
                strength = mass = conc = jnp.zeros((BLOCK, LANES), jnp.float32)
                for n in range(cats):
                    height = thick[n, pl.ds(r, BLOCK), lanes].astype(jnp.float32)
                    cover = jnp.where(limit > n, area[n, pl.ds(r, BLOCK), lanes].astype(jnp.float32), 0.0)
                    volume = cover * height
                    conc = conc + cover
                    mass = mass + volume
                    strength = strength + weight[n] * (volume * height)
                own[0, pl.ds(r, BLOCK), lanes] = strength
                own[1, pl.ds(r, BLOCK), lanes] = mass
                own[2, pl.ds(r, BLOCK), lanes] = conc
            return carry

        lax.fori_loop(0, count, body, 0)

    def exchange(slot, r0, height, c0, w):
        part = (pl.ds(0, 3), pl.ds(r0, height), pl.ds(c0, w))
        return pltpu.make_async_remote_copy(
            src_ref=own.at[part],
            dst_ref=other.at[part],
            send_sem=x_send.at[slot],
            recv_sem=x_recv.at[slot],
            device_id=partner,
            device_id_type=MESH,
        )

    def total(r0, count, c0, w):
        def body(i, carry):
            r = pl.multiple_of(r0 + i * BLOCK, BLOCK)
            for f in range(3):
                field[f, pl.ds(pl.multiple_of(r + TOP, 8), BLOCK), pl.ds(c0, w)] = (
                    own[f, pl.ds(r, BLOCK), pl.ds(c0, w)] + other[f, pl.ds(r, BLOCK), pl.ds(c0, w)]
                )
            return carry

        lax.fori_loop(0, count, body, 0)

    border = (
        (0, rows, 0, LANES),
        (0, rows, last, LANES),
        (0, BLOCK, LANES, middle),
        (rows - BLOCK, BLOCK, LANES, middle),
    )
    top_load.wait()
    for slot, (r0, height, c0, w) in enumerate(border):
        if slot < 3:
            for copy in cat_loads[slot]:
                copy.wait()
        partial(r0, height // BLOCK, c0, w)
        if slot == 0:
            pl.semaphore_wait(
                barrier, 3 + has_north.astype(jnp.int32) + has_south.astype(jnp.int32)
            )
        exchange(slot, r0, height, c0, w).start()

    def inner(e):
        return exchange(
            4 + e, pl.multiple_of(BLOCK + e * CHUNK, BLOCK), CHUNK, LANES, middle
        )

    def send_inner(e, carry):
        partial(BLOCK + e * CHUNK, CHUNK // BLOCK, LANES, middle)
        inner(e).start()
        return carry

    lax.fori_loop(0, events, send_inner, 0)

    land_load.wait()

    def wet_body(i, carry):
        r = pl.multiple_of(i * BLOCK, BLOCK)
        field[FW, pl.ds(pl.multiple_of(r + TOP, 8), BLOCK), pl.ds(0, cols)] = land[
            pl.ds(r, BLOCK), :
        ].astype(jnp.float32)
        return carry

    lax.fori_loop(0, rows // BLOCK, wet_body, 0)
    for copy in field_loads:
        copy.wait()

    for slot, (r0, height, c0, w) in enumerate(border):
        exchange(slot, r0, height, c0, w).wait_recv()
        total(r0, height // BLOCK, c0, w)

    def pack_body(i, carry):
        r = pl.multiple_of(i * CHUNK, 8)
        lane = lax.broadcasted_iota(jnp.int32, (CHUNK, LANES), 1)
        source = pl.ds(pl.multiple_of(r + TOP, 8), CHUNK)
        left = field[0, source, pl.ds(0, LANES)]
        right = field[0, source, pl.ds(last, LANES)]
        for f in range(1, FIELDS):
            x = field[f, source, pl.ds(0, LANES)]
            left = jnp.where(lane >= EDGE * f, pltpu.roll(x, EDGE * f, 1), left)
            y = field[f, source, pl.ds(last, LANES)]
            right = jnp.where(lane < LANES - EDGE * f, pltpu.roll(y, LANES - EDGE * f, 1), right)
        pack_left[pl.ds(r, CHUNK), :] = left
        pack_right[pl.ds(r, CHUNK), :] = right
        return carry

    lax.fori_loop(0, rows // CHUNK, pack_body, 0)
    to_east = pltpu.make_async_remote_copy(
        src_ref=pack_right,
        dst_ref=from_left,
        send_sem=halo_send.at[0],
        recv_sem=halo_recv.at[0],
        device_id=east,
        device_id_type=MESH,
    )
    to_west = pltpu.make_async_remote_copy(
        src_ref=pack_left,
        dst_ref=from_right,
        send_sem=halo_send.at[1],
        recv_sem=halo_recv.at[1],
        device_id=west,
        device_id_type=MESH,
    )
    to_east.start()
    to_west.start()
    to_east.wait()
    to_west.wait()

    def unpack_body(i, carry):
        r = pl.multiple_of(i * CHUNK, 8)
        lane = lax.broadcasted_iota(jnp.int32, (CHUNK, LANES), 1)
        x = from_right[pl.ds(r, CHUNK), :]
        y = from_left[pl.ds(r, CHUNK), :]
        for f in range(FIELDS):
            a = pltpu.roll(x, LANES - EDGE * f, 1) if f else x
            b = pltpu.roll(y, EDGE * f, 1) if f else y
            field[f, pl.ds(pl.multiple_of(r + TOP, 8), CHUNK), pl.ds(cols, LANES)] = jnp.where(
                lane < EDGE, a, jnp.where(lane >= LANES - EDGE, b, 0.0)
            )
        return carry

    lax.fori_loop(0, rows // CHUNK, unpack_body, 0)

    def row_copy(source, target, slot, device):
        return pltpu.make_async_remote_copy(
            src_ref=field.at[:, pl.ds(source, EDGE), :],
            dst_ref=field.at[:, pl.ds(target, EDGE), :],
            send_sem=halo_send.at[slot],
            recv_sem=halo_recv.at[slot],
            device_id=device,
            device_id_type=MESH,
        )

    to_north = row_copy(TOP, TOP + rows, 2, north)
    to_south = row_copy(TOP + rows - EDGE, TOP - EDGE, 3, south)

    @pl.when(has_north)
    def _():
        to_north.start()

    @pl.when(has_south)
    def _():
        to_south.start()

    @pl.when(has_north)
    def _():
        to_north.wait_send()
        to_south.wait_recv()

    @pl.when(has_south)
    def _():
        to_south.wait_send()
        to_north.wait_recv()

    third = 1.0 / 3.0

    def derive(i, carry):
        at = pl.ds(pl.multiple_of(BLOCK + i * BLOCK, 8), BLOCK)
        wet = field[FW, at, :]
        mass = field[FM, at, :]
        conc = field[FC, at, :]
        ratio = wet / (mass + field[FD, at, :] + 1.0 - wet)
        force = conc * ratio
        field[FS, at, :] = (2.0 * third) * wet * field[FS, at, :]
        field[FM, at, :] = mass * ratio
        field[FD, at, :] = 0.25 * ratio
        field[FX, at, :] = force * field[FX, at, :]
        field[FY, at, :] = force * field[FY, at, :]
        field[FW, at, :] = third * wet
        return carry

    tall = BLOCK + 2 * EDGE

    def rows_of(x):
        return x[EDGE : EDGE + BLOCK]

    def across(x):
        return rows_of(pltpu.roll(x, tall - 1, 0)) - rows_of(pltpu.roll(x, 1, 0))

    def along(x):
        return pltpu.roll(x, wide - 1, 1) - pltpu.roll(x, 1, 1)

    def stress(i, carry):
        r = BLOCK + i * BLOCK
        around = pl.ds(pl.multiple_of(r - EDGE, 8), tall)
        at = pl.ds(pl.multiple_of(r, 8), BLOCK)
        u = field[FU, around, :]
        v = field[FV, around, :]
        dxu, dyu = along(rows_of(u)), across(u)
        dxv, dyv = along(rows_of(v)), across(v)
        div = dxu + dyv
        ten = dxu - dyv
        shr = dyu + dxv
        inverse = lax.rsqrt(div * div + 0.25 * (ten * ten + shr * shr) + 0.01)
        power = field[FS, at, :]
        keep = field[FW, at, :]
        gain = power * inverse
        quarter = 0.25 * gain
        field[F1, at, :] = keep * field[F1, at, :] + (gain * div - power)
        field[F2, at, :] = keep * field[F2, at, :] + quarter * ten
        field[F3, at, :] = keep * field[F3, at, :] + quarter * shr
        return carry

    def motion(i, carry):
        r = EDGE + i * BLOCK
        around = pl.ds(pl.multiple_of(r - EDGE, 8), tall)
        at = pl.ds(pl.multiple_of(r, 8), BLOCK)
        first = field[F1, around, :]
        second = field[F2, around, :]
        cross = field[F3, around, :]
        total_x = rows_of(first) + rows_of(second)
        total_y = first - second
        bend = across(cross)
        fx = along(total_x) + (bend + bend)
        fy = along(rows_of(cross))
        fy = (fy + fy) + across(total_y)
        u = field[FU, at, :]
        v = field[FV, at, :]
        inertia = field[FM, at, :]
        ratio = field[FD, at, :]
        field[FU, at, :] = inertia * (u + 0.5 * v) + ratio * fx + field[FX, at, :]
        field[FV, at, :] = inertia * (v - 0.5 * u) + ratio * fy + field[FY, at, :]
        return carry

    blocks = (rows + 2 * EDGE) // BLOCK
    per = CHUNK // BLOCK

    def event(e, carry):
        inner(e).wait_recv()
        total(BLOCK + e * CHUNK, CHUNK // BLOCK, LANES, middle)
        first = e == 0
        final = e == events - 1

        def reach(lag, end):
            low = jnp.where(first, 0, 1 + per * e - lag)
            high = jnp.where(final, end, 3 + per * e - lag)
            return low, high

        low, high = reach(0, blocks)
        lax.fori_loop(low, high, derive, 0)

        def cycle(t, inner_carry):
            low, high = reach(t, blocks)
            lax.fori_loop(low, high, stress, 0)
            low, high = reach(t, blocks + 1)
            lax.fori_loop(low, high, motion, 0)
            return inner_carry

        lax.fori_loop(0, SUB, cycle, 0)
        return carry

    lax.fori_loop(0, events, event, 0)

    outs = []
    for k, (f, ref) in enumerate(
        ((FU, out_u), (FV, out_v), (F1, out_1), (F2, out_2), (F3, out_3))
    ):
        copy = pltpu.make_async_copy(
            field.at[f, pl.ds(TOP, rows), pl.ds(0, cols)], ref, out_sem.at[k]
        )
        copy.start()
        outs.append(copy)
    for slot, (r0, height, c0, w) in enumerate(border):
        exchange(slot, r0, height, c0, w).wait_send()

    def drain(e, carry):
        inner(e).wait_send()
        return carry

    lax.fori_loop(0, events, drain, 0)
    for copy in outs:
        copy.wait()


def shards(
    lat_count,
    lon_count,
    thickness,
    area,
    ridge_weight,
    cat_top,
    land_mask,
    velocity_u,
    velocity_v,
    stress_div,
    stress_ten,
    stress_shear,
    wind_x,
    wind_y,
    water_drag,
):
    cats, rows, cols = thickness.shape
    tall = rows + 2 * TOP
    wide = cols + LANES
    f32 = jnp.float32
    events = (rows - 2 * BLOCK) // CHUNK
    anywhere = pl.BlockSpec(memory_space=pl.ANY)
    return pl.pallas_call(
        functools.partial(kernel, lat_count, lon_count),
        out_shape=tuple(jax.ShapeDtypeStruct((rows, cols), f32) for _ in range(5)),
        in_specs=[pl.BlockSpec(memory_space=pltpu.SMEM)] + [anywhere] * 12,
        out_specs=tuple([anywhere] * 5),
        scratch_shapes=[
            pltpu.VMEM((FIELDS, tall, wide), f32),
            pltpu.VMEM((3, rows, cols), f32),
            pltpu.VMEM((3, rows, cols), f32),
            pltpu.VMEM((cats, rows, cols), thickness.dtype),
            pltpu.VMEM((cats, rows, cols), area.dtype),
            pltpu.VMEM((rows, cols), jnp.int32),
            pltpu.VMEM((rows, cols), jnp.int32),
            pltpu.VMEM((rows, LANES), f32),
            pltpu.VMEM((rows, LANES), f32),
            pltpu.VMEM((rows, LANES), f32),
            pltpu.VMEM((rows, LANES), f32),
            pltpu.SemaphoreType.DMA((16,)),
            pltpu.SemaphoreType.DMA((4 + events,)),
            pltpu.SemaphoreType.DMA((4 + events,)),
            pltpu.SemaphoreType.DMA((4,)),
            pltpu.SemaphoreType.DMA((4,)),
            pltpu.SemaphoreType.DMA((5,)),
        ],
        compiler_params=pltpu.CompilerParams(
            collective_id=0, has_side_effects=True, vmem_limit_bytes=56 * 2**20
        ),
        name="ice",
    )(
        ridge_weight,
        thickness,
        area,
        cat_top,
        land_mask,
        velocity_u,
        velocity_v,
        stress_div,
        stress_ten,
        stress_shear,
        wind_x,
        wind_y,
        water_drag,
    )


def solution(mesh):
    body = functools.partial(shards, mesh.shape["lat"], mesh.shape["lon"])
    plane = P("lat", "lon")
    return jax.shard_map(
        body,
        mesh=mesh,
        in_specs=(P("cat", "lat", "lon"), P("cat", "lat", "lon"), P("cat")) + (plane,) * 10,
        out_specs=(plane,) * 5,
        check_vma=False,
    )
```

time: 153 us -> 77.8 us (0.51)
  waiting for transfers between devices: 72.3 us -> 0 us
  Pallas kernels: 0 us -> 67 us
  other arithmetic: 42.8 us -> 0 us
  between operations: 14.4 us -> 0.65 us
  starting transfers between devices: 9.05 us -> 0 us
  local copies, waits for them, and re-layouts: 14.1 us -> 9.83 us
    pallas_call x0 -> x1, Pallas kernels: none -> 67 us  [shards(): pl.pallas_call(functools.partial(kernel, lat_count, lon_count), out_shape...]
    psum x1 -> x0, waiting for transfers between devices: 62.2 us -> none  [shards(): lax.psum((jnp.sum(weighted, axis=0), jnp.sum(cover * height, axis=0), jnp...]
    mul x22 -> x0, other arithmetic: 14 us -> none  [the longest x8 6.78 us: slopes(): 0.5 * (along[:, :, 2:] - along[:, :, :-2])]
    ppermute x4 -> x0, waiting for transfers between devices: 10.1 us -> none  [the longest x2 6.75 us: extended(): lax.ppermute(head, axis, [((i + 1) % count, i) for i in range(ends)])]
    reduce_sum x1 -> x0, other arithmetic: 9.63 us -> none  [shards(): jnp.sum(cover * height, axis=0)]
    ppermute x4 -> x0, starting transfers between devices: 9.01 us -> none  [the longest x2 5.01 us: extended(): lax.ppermute(tail, axis, [(i, (i + 1) % count) for i in range(ends)])]
    concatenate x1 -> x0, other arithmetic: 6.47 us -> none  [extended(): jnp.concatenate([lax.ppermute(tail, axis, [(i, (i + 1) % count) for i in...]
    squeeze x2 -> x0, other arithmetic: 4.95 us -> none  [shards(): return (velocity[0], velocity[1], stresses[0], stresses[1], stresses[2])]
  transfers between devices with their start and end apart: 5 -> 0, of which waited for: 5 -> 0; matrix products, arithmetic and copies ran while one was open for 1% -> 0% of each run, Pallas kernels for 0% -> 0%
where the time goes in v1:
time: 77.8 us; the launch traced here: 77.5 us
  Pallas kernels  67 us (86%)
  local copies, waits for them, and re-layouts  9.83 us (13%)
    pallas_call x1, Pallas kernels, shards(): pl.pallas_call(functools.partial(kernel, lat_count, lon_count), out_shape...  67 us
    unnamed x5, local copies, waits for them, and re-layouts  9.83 us

profile of v1, /device:TPU:1, one launch (start us, length us, event | category | flops | bytes accessed | tf_op | source)
XLA Modules:
  0.0 77.5 jit_solution(2072724184024366520)
XLA Ops:
  0.6 67.0 %ice.1 = (f32[256,640]{1,0:T(8,128)}, f32[256,640]{1,0:T(8,128)}, f32[256,640]{1,0:T(8,128)}, f32[256,640]{1,0:T(8,128)}, f32[256,640]{1,0:T(8,128)}) custom-call(f32[20]{0:T(128)} %weight.1, bf16[20,256,640]{2,1,0:T(8,128)(2,1)} %thick_hbm.1, bf16[20,256,640]{2,1,0:T(8,128)(2,1)} %area_hbm.1, s32[256,640]{1,0:T(8,128)} %top_hbm.1, s32[256,640]{1,0:T(8,128)} %land_hbm.1, ...), custom_call_target="tpu_custom_call" | custom-call | tf_op jit(solution)/shard_map/ice/pallas_call | solution.py:452
  67.6 2.0 %copy.23 = f32[256,640]{1,0:T(8,128)} copy(f32[256,640]{1,0:T(8,128)} %get-tuple-element.10) | data formatting | bytes 1310720
  69.6 2.0 %copy.24 = f32[256,640]{1,0:T(8,128)} copy(f32[256,640]{1,0:T(8,128)} %get-tuple-element.11) | data formatting | bytes 1310720
  71.6 2.0 %copy.25 = f32[256,640]{1,0:T(8,128)} copy(f32[256,640]{1,0:T(8,128)} %get-tuple-element.12) | data formatting | bytes 1310720
  73.5 2.0 %copy.26 = f32[256,640]{1,0:T(8,128)} copy(f32[256,640]{1,0:T(8,128)} %get-tuple-element.13) | data formatting | bytes 1310720
  75.5 2.0 %copy.27 = f32[256,640]{1,0:T(8,128)} copy(f32[256,640]{1,0:T(8,128)} %get-tuple-element.14) | data formatting | bytes 1310720

commit v2 on v1

--- a/solution.py
+++ b/solution.py
@@ -13,6 +13,7 @@
 CHUNK = 32
 BLOCK = 16
 TOP = 24
+FOLD = 4
 MESH = pl.DeviceIdType.MESH
 
 FS, FM, FC, FD, FX, FY, FW, FU, FV, F1, F2, F3 = range(12)
@@ -51,12 +52,15 @@
     pack_right,
     from_left,
     from_right,
+    sum_left,
+    sum_right,
+    sum_from_left,
+    sum_from_right,
     load_sem,
     x_send,
     x_recv,
     halo_send,
     halo_recv,
-    out_sem,
 ):
     cats, rows, cols = thick.shape
     wide = cols + LANES
@@ -219,92 +223,117 @@
     for copy in field_loads:
         copy.wait()
 
+    def lon_start(entries, buffers, slot):
+        left_out, right_out, left_in, right_in = buffers
+
+        def body(i, carry):
+            r = pl.multiple_of(i * CHUNK, 8)
+            lane = lax.broadcasted_iota(jnp.int32, (CHUNK, LANES), 1)
+            left = right = None
+            for k, (f, offset) in enumerate(entries):
+                source = pl.ds(pl.multiple_of(r + (TOP + offset), 8), CHUNK)
+                x = field[f, source, pl.ds(0, LANES)]
+                y = field[f, source, pl.ds(last, LANES)]
+                if k == 0:
+                    left, right = x, y
+                else:
+                    shift = EDGE * k
+                    left = jnp.where(lane >= shift, pltpu.roll(x, shift, 1), left)
+                    right = jnp.where(lane < LANES - shift, pltpu.roll(y, LANES - shift, 1), right)
+            left_out[pl.ds(r, CHUNK), :] = left
+            right_out[pl.ds(r, CHUNK), :] = right
+            return carry
+
+        lax.fori_loop(0, left_out.shape[0] // CHUNK, body, 0)
+        copies = tuple(
+            pltpu.make_async_remote_copy(
+                src_ref=source,
+                dst_ref=target,
+                send_sem=halo_send.at[slot + k],
+                recv_sem=halo_recv.at[slot + k],
+                device_id=device,
+                device_id_type=MESH,
+            )
+            for k, (source, target, device) in enumerate(
+                ((right_out, left_in, east), (left_out, right_in, west))
+            )
+        )
+        for copy in copies:
+            copy.start()
+        return copies
+
+    def lon_finish(entries, buffers, copies):
+        left_in, right_in = buffers[2:]
+        for copy in copies:
+            copy.wait()
+
+        def body(i, carry):
+            r = pl.multiple_of(i * CHUNK, 8)
+            lane = lax.broadcasted_iota(jnp.int32, (CHUNK, LANES), 1)
+            x = right_in[pl.ds(r, CHUNK), :]
+            y = left_in[pl.ds(r, CHUNK), :]
+            for k, (f, offset) in enumerate(entries):
+                a = pltpu.roll(x, LANES - EDGE * k, 1) if k else x
+                b = pltpu.roll(y, EDGE * k, 1) if k else y
+                target = pl.ds(pl.multiple_of(r + (TOP + offset), 8), CHUNK)
+                field[f, target, pl.ds(cols, LANES)] = jnp.where(
+                    lane < EDGE, a, jnp.where(lane >= LANES - EDGE, b, 0.0)
+                )
+            return carry
+
+        lax.fori_loop(0, left_in.shape[0] // CHUNK, body, 0)
+
+    def lat_start(first, count, slot):
+        def row_copy(source, target, at, device):
+            return pltpu.make_async_remote_copy(
+                src_ref=field.at[pl.ds(first, count), pl.ds(source, EDGE), :],
+                dst_ref=field.at[pl.ds(first, count), pl.ds(target, EDGE), :],
+                send_sem=halo_send.at[at],
+                recv_sem=halo_recv.at[at],
+                device_id=device,
+                device_id_type=MESH,
+            )
+
+        to_north = row_copy(TOP, TOP + rows, slot, north)
+        to_south = row_copy(TOP + rows - EDGE, TOP - EDGE, slot + 1, south)
+
+        @pl.when(has_north)
+        def _():
+            to_north.start()
+
+        @pl.when(has_south)
+        def _():
+            to_south.start()
+
+        return to_north, to_south
+
+    def lat_finish(to_north, to_south):
+        @pl.when(has_north)
+        def _():
+            to_north.wait_send()
+            to_south.wait_recv()
+
+        @pl.when(has_south)
+        def _():
+            to_south.wait_send()
+            to_north.wait_recv()
+
+    wide_pack = (pack_left, pack_right, from_left, from_right)
+    input_entries = [(f, 0) for f in range(3, FIELDS)]
+    input_copies = lon_start(input_entries, wide_pack, 0)
+    lon_finish(input_entries, wide_pack, input_copies)
+    input_rows = lat_start(3, FIELDS - 3, 2)
     for slot, (r0, height, c0, w) in enumerate(border):
         exchange(slot, r0, height, c0, w).wait_recv()
         total(r0, height // BLOCK, c0, w)
-
-    def pack_body(i, carry):
-        r = pl.multiple_of(i * CHUNK, 8)
-        lane = lax.broadcasted_iota(jnp.int32, (CHUNK, LANES), 1)
-        source = pl.ds(pl.multiple_of(r + TOP, 8), CHUNK)
-        left = field[0, source, pl.ds(0, LANES)]
-        right = field[0, source, pl.ds(last, LANES)]
-        for f in range(1, FIELDS):
-            x = field[f, source, pl.ds(0, LANES)]
-            left = jnp.where(lane >= EDGE * f, pltpu.roll(x, EDGE * f, 1), left)
-            y = field[f, source, pl.ds(last, LANES)]
-            right = jnp.where(lane < LANES - EDGE * f, pltpu.roll(y, LANES - EDGE * f, 1), right)
-        pack_left[pl.ds(r, CHUNK), :] = left
-        pack_right[pl.ds(r, CHUNK), :] = right
-        return carry
-
-    lax.fori_loop(0, rows // CHUNK, pack_body, 0)
-    to_east = pltpu.make_async_remote_copy(
-        src_ref=pack_right,
-        dst_ref=from_left,
-        send_sem=halo_send.at[0],
-        recv_sem=halo_recv.at[0],
-        device_id=east,
-        device_id_type=MESH,
-    )
-    to_west = pltpu.make_async_remote_copy(
-        src_ref=pack_left,
-        dst_ref=from_right,
-        send_sem=halo_send.at[1],
-        recv_sem=halo_recv.at[1],
-        device_id=west,
-        device_id_type=MESH,
-    )
-    to_east.start()
-    to_west.start()
-    to_east.wait()
-    to_west.wait()
-
-    def unpack_body(i, carry):
-        r = pl.multiple_of(i * CHUNK, 8)
-        lane = lax.broadcasted_iota(jnp.int32, (CHUNK, LANES), 1)
-        x = from_right[pl.ds(r, CHUNK), :]
-        y = from_left[pl.ds(r, CHUNK), :]
-        for f in range(FIELDS):
-            a = pltpu.roll(x, LANES - EDGE * f, 1) if f else x
-            b = pltpu.roll(y, EDGE * f, 1) if f else y
-            field[f, pl.ds(pl.multiple_of(r + TOP, 8), CHUNK), pl.ds(cols, LANES)] = jnp.where(
-                lane < EDGE, a, jnp.where(lane >= LANES - EDGE, b, 0.0)
-            )
-        return carry
-
-    lax.fori_loop(0, rows // CHUNK, unpack_body, 0)
-
-    def row_copy(source, target, slot, device):
-        return pltpu.make_async_remote_copy(
-            src_ref=field.at[:, pl.ds(source, EDGE), :],
-            dst_ref=field.at[:, pl.ds(target, EDGE), :],
-            send_sem=halo_send.at[slot],
-            recv_sem=halo_recv.at[slot],
-            device_id=device,
-            device_id_type=MESH,
-        )
-
-    to_north = row_copy(TOP, TOP + rows, 2, north)
-    to_south = row_copy(TOP + rows - EDGE, TOP - EDGE, 3, south)
-
-    @pl.when(has_north)
-    def _():
-        to_north.start()
-
-    @pl.when(has_south)
-    def _():
-        to_south.start()
-
-    @pl.when(has_north)
-    def _():
-        to_north.wait_send()
-        to_south.wait_recv()
-
-    @pl.when(has_south)
-    def _():
-        to_south.wait_send()
-        to_north.wait_recv()
+    short = rows // FOLD
+    sum_pack = (sum_left, sum_right, sum_from_left, sum_from_right)
+    sum_entries = [(f, g * short) for g in range(FOLD) for f in range(3)]
+    sum_copies = lon_start(sum_entries, sum_pack, 4)
+    lon_finish(sum_entries, sum_pack, sum_copies)
+    sum_rows = lat_start(0, 3, 6)
+    lat_finish(*input_rows)
+    lat_finish(*sum_rows)
 
     third = 1.0 / 3.0
 
@@ -323,25 +352,20 @@
         field[FW, at, :] = third * wet
         return carry
 
-    tall = BLOCK + 2 * EDGE
-
-    def rows_of(x):
-        return x[EDGE : EDGE + BLOCK]
-
-    def across(x):
-        return rows_of(pltpu.roll(x, tall - 1, 0)) - rows_of(pltpu.roll(x, 1, 0))
+    def near(f, r):
+        return field.at[f, pl.ds(pl.multiple_of(r - EDGE, 8), BLOCK + 2 * EDGE)]
+
+    def across(read):
+        return read(EDGE + 1, EDGE + 1 + BLOCK) - read(EDGE - 1, EDGE - 1 + BLOCK)
 
     def along(x):
         return pltpu.roll(x, wide - 1, 1) - pltpu.roll(x, 1, 1)
 
     def stress(i, carry):
-        r = BLOCK + i * BLOCK
-        around = pl.ds(pl.multiple_of(r - EDGE, 8), tall)
-        at = pl.ds(pl.multiple_of(r, 8), BLOCK)
-        u = field[FU, around, :]
-        v = field[FV, around, :]
-        dxu, dyu = along(rows_of(u)), across(u)
-        dxv, dyv = along(rows_of(v)), across(v)
+        r = pl.multiple_of(BLOCK + i * BLOCK, 8)
+        at = pl.ds(r, BLOCK)
+        dxu, dyu = along(field[FU, at, :]), across(lambda a, b: near(FU, r)[a:b, :])
+        dxv, dyv = along(field[FV, at, :]), across(lambda a, b: near(FV, r)[a:b, :])
         div = dxu + dyv
         ten = dxu - dyv
         shr = dyu + dxv
@@ -356,18 +380,12 @@
         return carry
 
     def motion(i, carry):
-        r = EDGE + i * BLOCK
-        around = pl.ds(pl.multiple_of(r - EDGE, 8), tall)
-        at = pl.ds(pl.multiple_of(r, 8), BLOCK)
-        first = field[F1, around, :]
-        second = field[F2, around, :]
-        cross = field[F3, around, :]
-        total_x = rows_of(first) + rows_of(second)
-        total_y = first - second
-        bend = across(cross)
-        fx = along(total_x) + (bend + bend)
-        fy = along(rows_of(cross))
-        fy = (fy + fy) + across(total_y)
+        r = pl.multiple_of(EDGE + i * BLOCK, 8)
+        at = pl.ds(r, BLOCK)
+        bend = across(lambda a, b: near(F3, r)[a:b, :])
+        fx = along(field[F1, at, :] + field[F2, at, :]) + (bend + bend)
+        fy = along(field[F3, at, :])
+        fy = (fy + fy) + across(lambda a, b: near(F1, r)[a:b, :] - near(F2, r)[a:b, :])
         u = field[FU, at, :]
         v = field[FV, at, :]
         inertia = field[FM, at, :]
@@ -405,15 +423,14 @@
 
     lax.fori_loop(0, events, event, 0)
 
-    outs = []
-    for k, (f, ref) in enumerate(
-        ((FU, out_u), (FV, out_v), (F1, out_1), (F2, out_2), (F3, out_3))
-    ):
-        copy = pltpu.make_async_copy(
-            field.at[f, pl.ds(TOP, rows), pl.ds(0, cols)], ref, out_sem.at[k]
-        )
-        copy.start()
-        outs.append(copy)
+    def deliver(i, carry):
+        r = pl.multiple_of(i * BLOCK, BLOCK)
+        source = pl.ds(pl.multiple_of(r + TOP, 8), BLOCK)
+        for f, ref in ((FU, out_u), (FV, out_v), (F1, out_1), (F2, out_2), (F3, out_3)):
+            ref[pl.ds(r, BLOCK), :] = field[f, source, pl.ds(0, cols)]
+        return carry
+
+    lax.fori_loop(0, rows // BLOCK, deliver, 0)
     for slot, (r0, height, c0, w) in enumerate(border):
         exchange(slot, r0, height, c0, w).wait_send()
 
@@ -422,7 +439,14 @@
         return carry
 
     lax.fori_loop(0, events, drain, 0)
-    for copy in outs:
+
+
+def write_out(*refs):
+    sem = refs[10]
+    copies = [pltpu.make_async_copy(refs[k], refs[5 + k], sem.at[k]) for k in range(5)]
+    for copy in copies:
+        copy.start()
+    for copy in copies:
         copy.wait()
 
 
@@ -449,11 +473,11 @@
     f32 = jnp.float32
     events = (rows - 2 * BLOCK) // CHUNK
     anywhere = pl.BlockSpec(memory_space=pl.ANY)
-    return pl.pallas_call(
+    results = pl.pallas_call(
         functools.partial(kernel, lat_count, lon_count),
-        out_shape=tuple(jax.ShapeDtypeStruct((rows, cols), f32) for _ in range(5)),
+        out_shape=tuple(pltpu.VMEM((rows, cols), f32) for _ in range(5)),
         in_specs=[pl.BlockSpec(memory_space=pltpu.SMEM)] + [anywhere] * 12,
-        out_specs=tuple([anywhere] * 5),
+        out_specs=tuple([pl.BlockSpec(memory_space=pltpu.VMEM)] * 5),
         scratch_shapes=[
             pltpu.VMEM((FIELDS, tall, wide), f32),
             pltpu.VMEM((3, rows, cols), f32),
@@ -466,15 +490,18 @@
             pltpu.VMEM((rows, LANES), f32),
             pltpu.VMEM((rows, LANES), f32),
             pltpu.VMEM((rows, LANES), f32),
+            pltpu.VMEM((rows // FOLD, LANES), f32),
+            pltpu.VMEM((rows // FOLD, LANES), f32),
+            pltpu.VMEM((rows // FOLD, LANES), f32),
+            pltpu.VMEM((rows // FOLD, LANES), f32),
             pltpu.SemaphoreType.DMA((16,)),
             pltpu.SemaphoreType.DMA((4 + events,)),
             pltpu.SemaphoreType.DMA((4 + events,)),
-            pltpu.SemaphoreType.DMA((4,)),
-            pltpu.SemaphoreType.DMA((4,)),
-            pltpu.SemaphoreType.DMA((5,)),
+            pltpu.SemaphoreType.DMA((8,)),
+            pltpu.SemaphoreType.DMA((8,)),
         ],
         compiler_params=pltpu.CompilerParams(
-            collective_id=0, has_side_effects=True, vmem_limit_bytes=56 * 2**20
+            collective_id=0, has_side_effects=True, vmem_limit_bytes=60 * 2**20
         ),
         name="ice",
     )(
@@ -492,6 +519,15 @@
         wind_y,
         water_drag,
     )
+    return pl.pallas_call(
+        write_out,
+        out_shape=tuple(jax.ShapeDtypeStruct((rows, cols), f32) for _ in range(5)),
+        in_specs=[pl.BlockSpec(memory_space=pltpu.VMEM)] * 5,
+        out_specs=(anywhere,) * 5,
+        scratch_shapes=[pltpu.SemaphoreType.DMA((5,))],
+        compiler_params=pltpu.CompilerParams(vmem_limit_bytes=4 * 2**20),
+        name="write_out",
+    )(*results)
 
 
 def solution(mesh):

time: 77.8 us -> 62.3 us (0.80)
  local copies, waits for them, and re-layouts: 9.83 us -> 0 us
  Pallas kernels: 67 us -> 61.4 us
    unnamed x5 -> x0, local copies, waits for them, and re-layouts: 9.83 us -> none
    pallas_call x1, Pallas kernels: 67 us -> 59.7 us  [shards(): pl.pallas_call(functools.partial(kernel, lat_count, lon_count), out_shape...]
    pallas_call x0 -> x1, Pallas kernels: none -> 1.75 us  [shards(): pl.pallas_call(write_out, out_shape=tuple((jax.ShapeDtypeStruct((rows, co...]
where the time goes in v2:
time: 62.3 us; the launch traced here: 62.1 us
  Pallas kernels  61.4 us (99%)
  between operations  0.64 us (1%)
    pallas_call x1, Pallas kernels, shards(): pl.pallas_call(functools.partial(kernel, lat_count, lon_count), out_shape...  59.7 us
    pallas_call x1, Pallas kernels, shards(): pl.pallas_call(write_out, out_shape=tuple((jax.ShapeDtypeStruct((rows, co...  1.75 us

profile of v2, /device:TPU:1, one launch (start us, length us, event | category | flops | bytes accessed | tf_op | source)
XLA Modules:
  0.0 62.1 jit_solution(2665215465781432341)
XLA Ops:
  0.6 59.7 %ice.1 = (f32[256,640]{1,0:T(8,128)S(1)}, f32[256,640]{1,0:T(8,128)S(1)}, f32[256,640]{1,0:T(8,128)S(1)}, f32[256,640]{1,0:T(8,128)S(1)}, f32[256,640]{1,0:T(8,128)S(1)}) custom-call(f32[20]{0:T(128)} %weight.1, bf16[20,256,640]{2,1,0:T(8,128)(2,1)} %thick_hbm.1, bf16[20,256,640]{2,1,0:T(8,128)(2,1)} %area_hbm.1, s32[256,640]{1,0:T(8,128)} %top_hbm.1, ...), custom_call_target="tpu_custom_call" | custom-call | tf_op jit(solution)/shard_map/ice/pallas_call | solution.py:476
  60.3 1.7 %write_out.1 = (f32[256,640]{1,0:T(8,128)}, f32[256,640]{1,0:T(8,128)}, f32[256,640]{1,0:T(8,128)}, f32[256,640]{1,0:T(8,128)}, f32[256,640]{1,0:T(8,128)}) custom-call(f32[256,640]{1,0:T(8,128)S(1)} %get-tuple-element.10.refs_0_, f32[256,640]{1,0:T(8,128)S(1)} %get-tuple-element.11.refs_1_, f32[256,640]{1,0:T(8,128)S(1)} %get-tuple-element.12.refs_2_, ...), custom_call_target="tpu_custom_call" | custom-call | tf_op jit(solution)/shard_map/write_out/pallas_call | solution.py:522
